TPU v7x, 256 devices: a whole 4x4x8 slice. The times are simulated.
256 devices in a mesh: grp: 4 (over y), cp: 64 (over x, z, core).
Axes of the slice: x: 4, y: 4, z: 8, core: 2. Of those that a mesh axis runs over, the one named last changes fastest.
Arguments:
- queries: bfloat16 [131072, 2048], P(('grp', 'cp')), parts along dimension 0, may hold values from -6 to 6
- keys: bfloat16 [131072, 1024], P(('grp', 'cp')), parts along dimension 0, may hold values from -8 to 8
- values: bfloat16 [131072, 1024], P(('grp', 'cp')), parts along dimension 0, may hold values from -6 to 6
- doc_lengths: int32 [1024], P('grp'), parts along dimension 0, may hold values from 1 to 1024, 32768 in all
Outputs:
- attended: bfloat16 [131072, 2048], P(('grp', 'cp')), parts along dimension 0
There are 4 independent parts, one for each index of `grp`. A program takes and returns all parts, laid end to end along the dimension named above; each array names one. Nothing has to cross between parts.
Inputs may be any that keep to these rules, and one draw needn't show every extreme that they name: doc_lengths sums to 32768, and its largest entry is exactly 1024.
All inputs are finite; a program needn't handle non-finite values.
Results may differ from a plain program's by a relative error of at most 0.0031.
Values may be sent and summed in bfloat16 or wider, within the bound.
A program may use at most 64 MiB of HBM per device.

v0:
```python
import functools
import math

import jax
import jax.numpy as jnp
from jax import lax
from jax.experimental import pallas as pl
from jax.experimental.pallas import tpu as pltpu
from jax.sharding import PartitionSpec as P

HQ = 16
HK = 8
DH = 128
REACH = 2
GROUPS = HQ // HK
WIDTH = GROUPS * DH
TILE = 128
MASKED = -1e30

exponent_scale = 144.0 ** (-0.5) * math.log2(math.e)


LOG2E = math.log2(math.e)
SPLIT = HK // 2
MESH = pl.DeviceIdType.MESH


def kernel(
    shards,
    lengths_ref,
    queries_ref,
    keys_ref,
    values_ref,
    out_ref,
    held,
    query_held,
    out_held,
    query_back,
    slot,
    stat_out,
    stat_in,
    bias,
    back_bias,
    load_sem,
    query_sem,
    out_sem,
    core_send,
    core_recv,
    query_send,
    query_recv,
    slot_send,
    slot_recv,
    relay_send,
    relay_recv,
    stat_send,
    stat_recv,
):
    me = lax.axis_index("cp")
    core = lax.rem(me, 2)
    even = core == 0
    odd = core == 1
    partner = me + 1 - 2 * core
    rows = keys_ref.shape[0]
    docs = lengths_ref.shape[0]
    tiles = rows // TILE
    window = REACH * rows + TILE
    own = pl.ds(REACH * rows, rows)
    near = pl.ds(rows, rows)
    far = pl.ds(0, rows)
    has_prev = me >= 2
    has_next = me < shards - 2
    chip_begin = (me - core) * rows
    next_begin = chip_begin + 2 * rows

    def loads(head):
        lanes = pl.ds(pl.multiple_of(head * DH, DH), DH)
        return (
            pltpu.make_async_copy(keys_ref.at[:, lanes], held.at[head, 0, own], load_sem.at[head, 0]),
            pltpu.make_async_copy(values_ref.at[:, lanes], held.at[head, 1, own], load_sem.at[head, 1]),
        )

    def query_load(head):
        lanes = pl.ds(pl.multiple_of(head * WIDTH, WIDTH), WIDTH)
        return pltpu.make_async_copy(queries_ref.at[:, lanes], query_held.at[head], query_sem.at[head])

    def out_store(head):
        lanes = pl.ds(pl.multiple_of(head * WIDTH, WIDTH), WIDTH)
        return pltpu.make_async_copy(out_held.at[head], out_ref.at[:, lanes], out_sem.at[head])

    def remote(source, target, send, recv, device):
        return pltpu.make_async_remote_copy(
            src_ref=source,
            dst_ref=target,
            send_sem=send,
            recv_sem=recv,
            device_id={"cp": device},
            device_id_type=MESH,
        )

    def to_core(head, region):
        return remote(
            held.at[head, :, own], held.at[head, :, region], core_send.at[head], core_recv.at[head], partner
        )

    def query_to_prev(step, side):
        return remote(
            query_held.at[side * SPLIT + step],
            query_back.at[step],
            query_send.at[side * SPLIT + step],
            query_recv.at[step],
            me - 2 + side,
        )

    def slot_to_next(step, region):
        return remote(
            slot.at[step],
            held.at[core * SPLIT + step, :, region],
            slot_send.at[step],
            slot_recv.at[step],
            me + 2,
        )

    def relay(step, source, target):
        head = core * SPLIT + step
        return remote(
            held.at[head, :, source], held.at[head, :, target], relay_send.at[step], relay_recv.at[step], partner
        )

    def stat_to_next(step, head):
        return remote(
            stat_out.at[step], stat_in.at[head], stat_send.at[step], stat_recv.at[head], me + 2 - core
        )

    @pl.loop(0, SPLIT)
    def _(step):
        query_load(step).start()
        query_load(SPLIT + step).start()

    @pl.loop(0, HK)
    def _(head):
        for copy in loads(head):
            copy.start()

    barrier = pltpu.get_barrier_semaphore()

    def greet(device):
        pl.semaphore_signal(barrier, inc=1, device_id={"cp": device}, device_id_type=MESH)

    greet(partner)

    @pl.when(has_prev)
    def _():
        greet(me - 2)

        @pl.when(even)
        def _():
            greet(me - 1)

    @pl.when(has_next)
    def _():
        greet(me + 2)

        @pl.when(odd)
        def _():
            greet(me + 1)

    back_peers = jnp.where(has_prev, 2 - core, 0)
    next_peers = jnp.where(has_next, 1 + core, 0)
    pl.semaphore_wait(barrier, 1 + back_peers + next_peers)

    @pl.loop(0, SPLIT)
    def _(step):
        for side in range(2):
            query_load(side * SPLIT + step).wait()

            @pl.when(jnp.logical_and(even, has_prev))
            def _():
                query_to_prev(step, side).start()

    @pl.loop(0, HK)
    def _(head):
        for copy in loads(head):
            copy.wait()

        @pl.when(even)
        def _():
            to_core(head, near).start()

        @pl.when(jnp.logical_and(odd, head < SPLIT))
        def _():
            to_core(head, far).start()

    @pl.when(jnp.logical_not(has_prev))
    def _():
        @pl.when(even)
        def _():
            held[:, :, near, :] = jnp.zeros((HK, 2, rows, DH), held.dtype)
            stat_in[...] = jnp.full(stat_in.shape, MASKED, jnp.float32)

        @pl.when(odd)
        def _():
            held[:, :, far, :] = jnp.zeros((HK, 2, rows, DH), held.dtype)

    def doc_begins(positions):
        def next_doc(doc, state):
            end, begins = state
            end = end + lengths_ref[doc]
            return end, jnp.maximum(begins, jnp.where(positions >= end, end, 0))

        start = (jnp.int32(0), jnp.zeros(positions.shape, jnp.int32))
        return lax.fori_loop(0, docs, next_doc, start)[1]

    def sends_keys(boundary):
        positions = jnp.full((1, DH), boundary, jnp.int32)
        return boundary - doc_begins(positions) <= rows

    row_iota = lax.broadcasted_iota(jnp.int32, (TILE, 1), 0)
    floor = jnp.where(sends_keys(chip_begin), 0, chip_begin)[:, :1]
    for tile in range(tiles):
        query_pos = me * rows + tile * TILE + row_iota
        begins = jnp.maximum(doc_begins(query_pos), floor)
        first = jnp.where(even, (me - 1) * rows, (me - 2) * rows + tile * TILE)
        key_pos = first + lax.broadcasted_iota(jnp.int32, (TILE, window), 1)
        visible = (key_pos >= begins) & (key_pos <= query_pos)
        bias[pl.ds(tile * TILE, TILE), :] = jnp.where(visible, 0.0, MASKED)

    for tile in range(tiles):
        begins = doc_begins(next_begin + tile * TILE + row_iota)
        key_pos = chip_begin + lax.broadcasted_iota(jnp.int32, (TILE, 2 * rows), 1)
        back_bias[pl.ds(tile * TILE, TILE), :] = jnp.where(key_pos >= begins, 0.0, MASKED)

    next_keys = sends_keys(next_begin)
    diagonal = lax.broadcasted_iota(jnp.int32, (TILE, TILE), 0) == lax.broadcasted_iota(
        jnp.int32, (TILE, TILE), 1
    )

    def stack(queries):
        return jnp.concatenate([queries[:, g * DH : (g + 1) * DH] for g in range(GROUPS)], axis=0)

    def dot_keys(queries, keys):
        return lax.dot_general(
            queries, keys, (((1,), (1,)), ((), ())), preferred_element_type=jnp.float32
        )

    def softmax(scores, mask):
        scores = scores.reshape(GROUPS, TILE, scores.shape[-1]) * exponent_scale + mask[None]
        highest = jnp.max(scores, axis=-1, keepdims=True)
        weights = jnp.exp2(scores - highest)
        totals = jnp.sum(weights, axis=-1, keepdims=True)
        rounded = weights.astype(jnp.bfloat16).reshape(GROUPS * TILE, scores.shape[-1])
        return highest, totals, rounded

    def dot_values(weights, values):
        return jnp.dot(weights, values, preferred_element_type=jnp.float32)

    def attend_back(step):
        head = core * SPLIT + step
        older = pl.multiple_of((2 - core) * rows, TILE)
        newer = pl.multiple_of(2 * core * rows, TILE)
        newer_rows = pl.ds(newer, rows)
        for tile in range(tiles):
            span = pl.ds(tile * TILE, TILE)
            count = rows - tile * TILE
            older_rows = pl.ds(older + tile * TILE, count)
            queries = stack(query_back[step, span, :])
            scores = jnp.concatenate(
                [
                    dot_keys(queries, held[head, 0, older_rows, :]),
                    dot_keys(queries, held[head, 0, newer_rows, :]),
                ],
                axis=1,
            )
            highest, totals, weights = softmax(scores, back_bias[span, pl.ds(tile * TILE, count + rows)])
            mixed = dot_values(weights[:, :count], held[head, 1, older_rows, :]) + dot_values(
                weights[:, count:], held[head, 1, newer_rows, :]
            )
            mixed = mixed.reshape(GROUPS, TILE, DH) / totals
            level = highest + jnp.log(totals) * LOG2E
            sent = pl.ds(newer + tile * TILE, TILE)
            for g in range(GROUPS):
                kept = held[head, g, sent, :].astype(jnp.float32)
                slot[step, g, span, :] = jnp.where(next_keys, kept, mixed[g]).astype(jnp.bfloat16)
                row = jnp.sum(jnp.where(diagonal, level[g], 0.0), axis=0, keepdims=True)
                stat_out[step, pl.ds(tile * GROUPS + g, 1), :] = jnp.where(next_keys, MASKED, row)

    def attend_even(head):
        for tile in range(tiles):
            span = pl.ds(tile * TILE, TILE)
            count = rows + (tile + 1) * TILE
            keys = pl.ds(rows, count)
            scores = dot_keys(stack(query_held[head, span, :]), held[head, 0, keys, :])
            highest, totals, weights = softmax(scores, bias[span, pl.ds(0, count)])
            mixed = dot_values(weights, held[head, 1, keys, :]).reshape(GROUPS, TILE, DH)
            for g in range(GROUPS):
                row = stat_in[head, pl.ds(tile * GROUPS + g, 1), :]
                level = jnp.sum(jnp.where(diagonal, row, 0.0), axis=1, keepdims=True)
                top = jnp.maximum(highest[g], level)
                here = jnp.exp2(highest[g] - top)
                there = jnp.exp2(level - top)
                partial = held[head, g, pl.ds(rows + tile * TILE, TILE), :].astype(jnp.float32)
                both = (mixed[g] * here + partial * there) / (totals[g] * here + there)
                out_held[head, span, pl.ds(g * DH, DH)] = both.astype(jnp.bfloat16)

    def attend_odd(head):
        for tile in range(tiles):
            span = pl.ds(tile * TILE, TILE)
            keys = pl.ds(tile * TILE, window)
            scores = dot_keys(stack(query_held[head, span, :]), held[head, 0, keys, :])
            _, totals, weights = softmax(scores, bias[span, :])
            mixed = dot_values(weights, held[head, 1, keys, :]).reshape(GROUPS, TILE, DH)
            mixed = (mixed / totals).astype(jnp.bfloat16)
            for g in range(GROUPS):
                out_held[head, span, pl.ds(g * DH, DH)] = mixed[g]

    @pl.when(even)
    def _():
        @pl.loop(0, SPLIT)
        def _(head):
            to_core(head, far).wait_recv()

    @pl.when(odd)
    def _():
        @pl.loop(0, HK)
        def _(head):
            to_core(head, near).wait_recv()

    @pl.loop(0, SPLIT + 1)
    def _(turn):
        @pl.when(jnp.logical_and(has_next, turn < SPLIT))
        def _():
            query_to_prev(turn, 0).wait_recv()
            attend_back(turn)

            @pl.when(even)
            def _():
                slot_to_next(turn, near).start()

            @pl.when(odd)
            def _():
                slot_to_next(turn, far).start()

            stat_to_next(turn, core * SPLIT + turn).start()

        @pl.when(turn >= 1)
        def _():
            step = turn - 1

            @pl.when(has_prev)
            def _():
                slot_to_next(step, far).wait_recv()

                @pl.when(even)
                def _():
                    relay(step, near, far).start()

                @pl.when(odd)
                def _():
                    relay(step, far, near).start()

            @pl.loop(0, 2)
            def _(turn_side):
                side = lax.rem(core + turn_side, 2)
                head = side * SPLIT + step

                @pl.when(jnp.logical_and(has_prev, turn_side == 1))
                def _():
                    relay(step, near, far).wait_recv()

                @pl.when(even)
                def _():
                    @pl.when(has_prev)
                    def _():
                        stat_to_next(step, head).wait_recv()

                    attend_even(head)

                @pl.when(odd)
                def _():
                    attend_odd(head)

                out_store(head).start()

    @pl.loop(0, HK)
    def _(head):
        out_store(head).wait()

        @pl.when(jnp.logical_or(even, head < SPLIT))
        def _():
            to_core(head, near).wait_send()

    @pl.loop(0, SPLIT)
    def _(step):
        @pl.when(has_next)
        def _():
            slot_to_next(step, near).wait_send()
            stat_to_next(step, step).wait_send()

        @pl.when(has_prev)
        def _():
            relay(step, near, far).wait_send()

            @pl.when(even)
            def _():
                for side in range(2):
                    query_to_prev(step, side).wait_send()


def on_device(queries, keys, values, doc_lengths):
    rows = keys.shape[0]
    shards = lax.axis_size("cp")
    window = REACH * rows + TILE
    stats = rows // TILE * GROUPS
    dma = pltpu.SemaphoreType.DMA
    return pl.pallas_call(
        functools.partial(kernel, shards),
        out_shape=jax.ShapeDtypeStruct(queries.shape, queries.dtype),
        in_specs=[
            pl.BlockSpec(memory_space=pltpu.SMEM),
            pl.BlockSpec(memory_space=pl.ANY),
            pl.BlockSpec(memory_space=pl.ANY),
            pl.BlockSpec(memory_space=pl.ANY),
        ],
        out_specs=pl.BlockSpec(memory_space=pl.ANY),
        scratch_shapes=[
            pltpu.VMEM((HK, 2, (REACH + 1) * rows, DH), keys.dtype),
            pltpu.VMEM((HK, rows, WIDTH), queries.dtype),
            pltpu.VMEM((HK, rows, WIDTH), queries.dtype),
            pltpu.VMEM((SPLIT, rows, WIDTH), queries.dtype),
            pltpu.VMEM((SPLIT, 2, rows, DH), keys.dtype),
            pltpu.VMEM((SPLIT, stats, TILE), jnp.float32),
            pltpu.VMEM((HK, stats, TILE), jnp.float32),
            pltpu.VMEM((rows, window), jnp.float32),
            pltpu.VMEM((rows, REACH * rows), jnp.float32),
            dma((HK, 2)),
            dma((HK,)),
            dma((HK,)),
            dma((HK,)),
            dma((HK,)),
            dma((HK,)),
            dma((SPLIT,)),
            dma((SPLIT,)),
            dma((SPLIT,)),
            dma((SPLIT,)),
            dma((SPLIT,)),
            dma((SPLIT,)),
            dma((HK,)),
        ],
        compiler_params=pltpu.CompilerParams(
            collective_id=0, has_side_effects=True, vmem_limit_bytes=58 * 1024 * 1024
        ),
    )(doc_lengths, queries, keys, values)


def solution(mesh):
    return jax.shard_map(
        on_device,
        mesh=mesh,
        in_specs=(P(("grp", "cp"), None), P(("grp", "cp"), None), P(("grp", "cp"), None), P("grp")),
        out_specs=P(("grp", "cp"), None),
        check_vma=False,
    )
```

profile of v0, /device:TPU:15, one launch (start us, length us, event | category | flops | bytes accessed | tf_op | source)
XLA Modules:
  0.0 87.0 jit_solution(5359322389903172132)
XLA Ops:
  0.0 83.9 %shard_map.46 = bf16[512,2048]{1,0:T(8,128)(2,1)} custom-call(s32[256]{0:T(256)} %lengths_ref.1, bf16[512,2048]{1,0:T(8,128)(2,1)} %queries_ref.1, bf16[512,1024]{1,0:T(8,128)(2,1)} %keys_ref.1, bf16[512,1024]{1,0:T(8,128)(2,1)} %values_ref.1), custom_call_target="tpu_custom_call" | custom-call | tf_op jit(solution)/shard_map/pallas_call | solution.py:414
  83.9 3.2 %copy.6 = bf16[512,2048]{1,0:T(8,128)(2,1)} copy(bf16[512,2048]{1,0:T(8,128)(2,1)} %shard_map.46) | data formatting | bytes 4194304
where the time goes:
time: 87.2 us; the launch traced here: 87 us
  Pallas kernels  83.9 us (96%)
  local copies, waits for them, and re-layouts  3.16 us (4%)
    pallas_call x1, Pallas kernels, on_device(): pl.pallas_call(functools.partial(kernel, shards), out_shape=jax.ShapeDtyp...  83.9 us
    unnamed x1, local copies, waits for them, and re-layouts  3.16 us

commit v1 on v0

--- a/solution.py
+++ b/solution.py
@@ -22,6 +22,11 @@
 
 LOG2E = math.log2(math.e)
 SPLIT = HK // 2
+MODULUS = 63
+APART = 65536.0
+SCORE_KEYS = 640
+MIX_KEYS = 256
+MIX_STEP = 64
 MESH = pl.DeviceIdType.MESH
 
 
@@ -39,8 +44,10 @@
     slot,
     stat_out,
     stat_in,
-    bias,
-    back_bias,
+    turned,
+    key_marks,
+    query_marks,
+    scores,
     load_sem,
     query_sem,
     out_sem,
@@ -201,142 +208,239 @@
         def _():
             held[:, :, far, :] = jnp.zeros((HK, 2, rows, DH), held.dtype)
 
-    def doc_begins(positions):
-        def next_doc(doc, state):
-            end, begins = state
-            end = end + lengths_ref[doc]
-            return end, jnp.maximum(begins, jnp.where(positions >= end, end, 0))
-
-        start = (jnp.int32(0), jnp.zeros(positions.shape, jnp.int32))
-        return lax.fori_loop(0, docs, next_doc, start)[1]
-
-    def sends_keys(boundary):
-        positions = jnp.full((1, DH), boundary, jnp.int32)
-        return boundary - doc_begins(positions) <= rows
-
-    row_iota = lax.broadcasted_iota(jnp.int32, (TILE, 1), 0)
-    floor = jnp.where(sends_keys(chip_begin), 0, chip_begin)[:, :1]
-    for tile in range(tiles):
-        query_pos = me * rows + tile * TILE + row_iota
-        begins = jnp.maximum(doc_begins(query_pos), floor)
-        first = jnp.where(even, (me - 1) * rows, (me - 2) * rows + tile * TILE)
-        key_pos = first + lax.broadcasted_iota(jnp.int32, (TILE, window), 1)
-        visible = (key_pos >= begins) & (key_pos <= query_pos)
-        bias[pl.ds(tile * TILE, TILE), :] = jnp.where(visible, 0.0, MASKED)
-
-    for tile in range(tiles):
-        begins = doc_begins(next_begin + tile * TILE + row_iota)
-        key_pos = chip_begin + lax.broadcasted_iota(jnp.int32, (TILE, 2 * rows), 1)
-        back_bias[pl.ds(tile * TILE, TILE), :] = jnp.where(key_pos >= begins, 0.0, MASKED)
-
-    next_keys = sends_keys(next_begin)
-    diagonal = lax.broadcasted_iota(jnp.int32, (TILE, TILE), 0) == lax.broadcasted_iota(
-        jnp.int32, (TILE, TILE), 1
+    row = lax.broadcasted_iota(jnp.int32, (4 * tiles, TILE), 0)
+    lane = lax.broadcasted_iota(jnp.int32, (4 * tiles, TILE), 1)
+    far_begin = jnp.where(even, me + 1, me - 2) * rows
+    region_begin = jnp.where(
+        row < tiles,
+        far_begin,
+        jnp.where(
+            row < 2 * tiles,
+            (me - 1) * rows - rows,
+            jnp.where(row < 3 * tiles, me * rows - 2 * rows, next_begin - 3 * rows),
+        ),
     )
-
-    def stack(queries):
-        return jnp.concatenate([queries[:, g * DH : (g + 1) * DH] for g in range(GROUPS)], axis=0)
-
-    def dot_keys(queries, keys):
-        return lax.dot_general(
-            queries, keys, (((1,), (1,)), ((), ())), preferred_element_type=jnp.float32
-        )
-
-    def softmax(scores, mask):
-        scores = scores.reshape(GROUPS, TILE, scores.shape[-1]) * exponent_scale + mask[None]
-        highest = jnp.max(scores, axis=-1, keepdims=True)
-        weights = jnp.exp2(scores - highest)
-        totals = jnp.sum(weights, axis=-1, keepdims=True)
-        rounded = weights.astype(jnp.bfloat16).reshape(GROUPS * TILE, scores.shape[-1])
-        return highest, totals, rounded
-
-    def dot_values(weights, values):
-        return jnp.dot(weights, values, preferred_element_type=jnp.float32)
-
-    def attend_back(step):
-        head = core * SPLIT + step
-        older = pl.multiple_of((2 - core) * rows, TILE)
-        newer = pl.multiple_of(2 * core * rows, TILE)
-        newer_rows = pl.ds(newer, rows)
+    positions = region_begin + row * TILE + lane
+    edge_row = lax.broadcasted_iota(jnp.int32, (8, TILE), 0)
+    edges = jnp.where(edge_row == 0, chip_begin, next_begin)
+
+    def next_docs(step, state):
+        end, doc, begins = state
+        for k in range(8):
+            end = end + lengths_ref[step * 8 + k]
+            doc = doc + (positions >= end).astype(jnp.int32)
+            begins = jnp.where(edges >= end, end, begins)
+        return end, doc, begins
+
+    _, doc, begins = lax.fori_loop(
+        0,
+        docs // 8,
+        next_docs,
+        (jnp.int32(0), jnp.zeros(positions.shape, jnp.int32), jnp.zeros(edges.shape, jnp.int32)),
+    )
+    sends_keys = (edges - begins <= rows).astype(jnp.int32)
+    next_keys = jnp.broadcast_to(sends_keys[1:2, :], (TILE, DH)) > 0
+    prev_keys = jnp.broadcast_to(sends_keys[0:1, :], positions.shape)
+    prev_row = jnp.where(even, 1, 0)
+    from_prev = (row >= prev_row * tiles) & (row < (prev_row + 1) * tiles)
+    none = (positions < 0) | (from_prev & (prev_keys == 0))
+    rest = doc
+    for k in range(1, docs // MODULUS + 1):
+        rest = rest - jnp.where(doc >= k * MODULUS, MODULUS, 0)
+    code_low = jnp.where(none, 2 * DH, doc & (DH // 2 - 1))
+    code_high = jnp.where(none, 2 * DH, rest + DH // 2)
+    feature = lax.broadcasted_iota(jnp.int32, (DH, TILE), 0)
+
+    def matches(block):
+        return (feature == code_low[block : block + 1, :]) | (feature == code_high[block : block + 1, :])
+
+    for block in range(3 * tiles):
+        missing = jnp.where(matches(block), 0.0, -APART).astype(jnp.bfloat16)
+        key_marks[pl.ds(block * TILE, TILE), :] = missing.T
+    for block in range(2 * tiles):
+        present = jnp.where(matches(2 * tiles + block), 1.0, 0.0).astype(jnp.bfloat16)
+        query_marks[:, pl.ds(block * TILE, TILE)] = present
+
+    causal = lax.broadcasted_iota(jnp.int32, (TILE, WIDTH), 0) <= lax.rem(
+        lax.broadcasted_iota(jnp.int32, (TILE, WIDTH), 1), TILE
+    )
+
+    def turn_values(head, region):
+        for tile in range(tiles):
+            span = pl.ds(region + tile * TILE, TILE)
+            turned[head, :, span] = held[head, 1, span, :].T
+
+    def pieces(spans, size):
+        cut, at = [], 0
+        for begin, count in spans:
+            done = 0
+            while done < count:
+                step = min(size, count - done)
+                cut.append((begin + done, at, step))
+                done, at = done + step, at + step
+        return cut
+
+    def score_job(job, buffer):
+        head, queries, marks, spans, own_end, _ = job
+        state = {"highest": None, "buffer": buffer}
+        turned_queries = jnp.concatenate([queries[:, g * DH : (g + 1) * DH].T for g in range(GROUPS)], axis=1)
+        right = jnp.concatenate([turned_queries, jnp.concatenate([marks] * GROUPS, axis=1)], axis=0)
+        total = sum(count for _, count in spans)
+
+        def piece(begin, at, count):
+            span = pl.ds(begin, count)
+            left = jnp.concatenate([held[head, 0, span, :], key_marks[span, :]], axis=1)
+            part = jnp.dot(left, right, preferred_element_type=jnp.float32)
+            if own_end and at + count == total:
+                last = jnp.where(causal, part[count - TILE :], -APART)
+                part = jnp.concatenate([part[: count - TILE], last], axis=0) if count > TILE else last
+            scores[buffer, pl.ds(at, count), :] = part
+            top = jnp.max(part.reshape(count // 8, 8, WIDTH), axis=0)
+            state["highest"] = top if state["highest"] is None else jnp.maximum(state["highest"], top)
+
+        def finish():
+            state["row"] = jnp.max(state["highest"], axis=0, keepdims=True)
+
+        return state, [functools.partial(piece, *cut) for cut in pieces(spans, SCORE_KEYS)], finish
+
+    def mix_job(job, state):
+        head, _, _, spans, _, store = job
+        buffer, highest = state["buffer"], state["row"]
+        sums = {"totals": None, "mixed": None}
+
+        def piece(begin, at, count):
+            span = pl.ds(begin, count)
+            rounded = []
+            for sub in range(0, count, MIX_STEP):
+                part = scores[buffer, pl.ds(at + sub, MIX_STEP), :]
+                weights = jnp.exp2((part - highest) * exponent_scale)
+                total = jnp.sum(weights.reshape(MIX_STEP // 8, 8, WIDTH), axis=0)
+                sums["totals"] = total if sums["totals"] is None else sums["totals"] + total
+                rounded.append(weights.astype(jnp.bfloat16))
+            mixed = jnp.dot(
+                turned[head, :, span], jnp.concatenate(rounded, axis=0), preferred_element_type=jnp.float32
+            )
+            sums["mixed"] = mixed if sums["mixed"] is None else sums["mixed"] + mixed
+
+        def finish():
+            totals = jnp.sum(sums["totals"], axis=0, keepdims=True)
+            store(highest * exponent_scale, totals, sums["mixed"])
+
+        return [functools.partial(piece, *cut) for cut in pieces(spans, MIX_KEYS)], finish
+
+    def run(jobs):
+        before = None
+        for index, job in enumerate(jobs + [None]):
+            state, score, score_end, mix, mix_end = None, [], None, [], None
+            if job is not None:
+                state, score, score_end = score_job(job, index % scores.shape[0])
+            if before is not None:
+                mix, mix_end = mix_job(*before)
+            for step in range(max(len(score), len(mix))):
+                if step < len(score):
+                    score[step]()
+                if step < len(mix):
+                    mix[step]()
+            if mix_end is not None:
+                mix_end()
+            if score_end is not None:
+                score_end()
+            before = (job, state)
+
+    def attend_back(head, step, older, newer):
+        jobs = []
         for tile in range(tiles):
             span = pl.ds(tile * TILE, TILE)
-            count = rows - tile * TILE
-            older_rows = pl.ds(older + tile * TILE, count)
-            queries = stack(query_back[step, span, :])
-            scores = jnp.concatenate(
-                [
-                    dot_keys(queries, held[head, 0, older_rows, :]),
-                    dot_keys(queries, held[head, 0, newer_rows, :]),
-                ],
-                axis=1,
-            )
-            highest, totals, weights = softmax(scores, back_bias[span, pl.ds(tile * TILE, count + rows)])
-            mixed = dot_values(weights[:, :count], held[head, 1, older_rows, :]) + dot_values(
-                weights[:, count:], held[head, 1, newer_rows, :]
-            )
-            mixed = mixed.reshape(GROUPS, TILE, DH) / totals
-            level = highest + jnp.log(totals) * LOG2E
-            sent = pl.ds(newer + tile * TILE, TILE)
-            for g in range(GROUPS):
-                kept = held[head, g, sent, :].astype(jnp.float32)
-                slot[step, g, span, :] = jnp.where(next_keys, kept, mixed[g]).astype(jnp.bfloat16)
-                row = jnp.sum(jnp.where(diagonal, level[g], 0.0), axis=0, keepdims=True)
-                stat_out[step, pl.ds(tile * GROUPS + g, 1), :] = jnp.where(next_keys, MASKED, row)
+
+            def store(level, totals, mixed, tile=tile, span=span):
+                mixed = (mixed * (1.0 / totals)).astype(jnp.bfloat16)
+                level = level + jnp.log(totals) * LOG2E
+                sent = pl.ds(newer + tile * TILE, TILE)
+                for g in range(GROUPS):
+                    part = pl.ds(g * DH, DH)
+                    turned_back = mixed[:, g * DH : (g + 1) * DH].T
+                    slot[step, g, span, :] = jnp.where(next_keys, held[head, g, sent, :], turned_back)
+                    stat_out[step, pl.ds(tile * GROUPS + g, 1), :] = jnp.where(
+                        next_keys[:1, :], MASKED, level[:, g * DH : (g + 1) * DH]
+                    )
+
+            spans = [(older + tile * TILE, rows - tile * TILE), (newer, rows)]
+            marks = query_marks[:, pl.ds(rows + tile * TILE, TILE)]
+            jobs.append((head, query_back[step, span, :], marks, spans, False, store))
+        run(jobs)
+
+    def put(head, span, mixed):
+        for g in range(GROUPS):
+            out_held[head, span, pl.ds(g * DH, DH)] = mixed[:, g * DH : (g + 1) * DH].T
 
     def attend_even(head):
+        jobs = []
         for tile in range(tiles):
             span = pl.ds(tile * TILE, TILE)
-            count = rows + (tile + 1) * TILE
-            keys = pl.ds(rows, count)
-            scores = dot_keys(stack(query_held[head, span, :]), held[head, 0, keys, :])
-            highest, totals, weights = softmax(scores, bias[span, pl.ds(0, count)])
-            mixed = dot_values(weights, held[head, 1, keys, :]).reshape(GROUPS, TILE, DH)
-            for g in range(GROUPS):
-                row = stat_in[head, pl.ds(tile * GROUPS + g, 1), :]
-                level = jnp.sum(jnp.where(diagonal, row, 0.0), axis=1, keepdims=True)
-                top = jnp.maximum(highest[g], level)
-                here = jnp.exp2(highest[g] - top)
-                there = jnp.exp2(level - top)
-                partial = held[head, g, pl.ds(rows + tile * TILE, TILE), :].astype(jnp.float32)
-                both = (mixed[g] * here + partial * there) / (totals[g] * here + there)
-                out_held[head, span, pl.ds(g * DH, DH)] = both.astype(jnp.bfloat16)
+
+            def store(level, totals, mixed, tile=tile, span=span):
+                sent = pl.ds(rows + tile * TILE, TILE)
+                other = jnp.concatenate(
+                    [stat_in[head, pl.ds(tile * GROUPS + g, 1), :] for g in range(GROUPS)], axis=1
+                )
+                top = jnp.maximum(level, other)
+                here = jnp.exp2(level - top)
+                there = jnp.exp2(other - top)
+                share = 1.0 / (totals * here + there)
+                partial = jnp.concatenate([held[head, 0, sent, :].T, turned[head, :, sent]], axis=1)
+                both = mixed * (here * share) + partial.astype(jnp.float32) * (there * share)
+                put(head, span, both.astype(jnp.bfloat16))
+
+            spans = [(rows, rows + (tile + 1) * TILE)]
+            marks = query_marks[:, span]
+            jobs.append((head, query_held[head, span, :], marks, spans, True, store))
+        run(jobs)
 
     def attend_odd(head):
+        jobs = []
         for tile in range(tiles):
             span = pl.ds(tile * TILE, TILE)
-            keys = pl.ds(tile * TILE, window)
-            scores = dot_keys(stack(query_held[head, span, :]), held[head, 0, keys, :])
-            _, totals, weights = softmax(scores, bias[span, :])
-            mixed = dot_values(weights, held[head, 1, keys, :]).reshape(GROUPS, TILE, DH)
-            mixed = (mixed / totals).astype(jnp.bfloat16)
-            for g in range(GROUPS):
-                out_held[head, span, pl.ds(g * DH, DH)] = mixed[g]
+
+            def store(level, totals, mixed, span=span):
+                put(head, span, (mixed * (1.0 / totals)).astype(jnp.bfloat16))
+
+            spans = [(tile * TILE, REACH * rows + TILE)]
+            marks = query_marks[:, span]
+            jobs.append((head, query_held[head, span, :], marks, spans, True, store))
+        run(jobs)
+
+    @pl.loop(0, HK)
+    def _(head):
+        turn_values(head, REACH * rows)
 
     @pl.when(even)
     def _():
         @pl.loop(0, SPLIT)
         def _(head):
             to_core(head, far).wait_recv()
+            turn_values(head, 0)
 
     @pl.when(odd)
     def _():
         @pl.loop(0, HK)
         def _(head):
             to_core(head, near).wait_recv()
+            turn_values(head, rows)
 
     @pl.loop(0, SPLIT + 1)
     def _(turn):
         @pl.when(jnp.logical_and(has_next, turn < SPLIT))
         def _():
             query_to_prev(turn, 0).wait_recv()
-            attend_back(turn)
 
             @pl.when(even)
             def _():
+                attend_back(turn, turn, 2 * rows, 0)
                 slot_to_next(turn, near).start()
 
             @pl.when(odd)
             def _():
+                attend_back(SPLIT + turn, turn, rows, 2 * rows)
                 slot_to_next(turn, far).start()
 
             stat_to_next(turn, core * SPLIT + turn).start()
@@ -372,10 +476,12 @@
                     def _():
                         stat_to_next(step, head).wait_recv()
 
+                    turn_values(head, rows)
                     attend_even(head)
 
                 @pl.when(odd)
                 def _():
+                    turn_values(head, 0)
                     attend_odd(head)
 
                 out_store(head).start()
@@ -429,8 +535,10 @@
             pltpu.VMEM((SPLIT, 2, rows, DH), keys.dtype),
             pltpu.VMEM((SPLIT, stats, TILE), jnp.float32),
             pltpu.VMEM((HK, stats, TILE), jnp.float32),
-            pltpu.VMEM((rows, window), jnp.float32),
-            pltpu.VMEM((rows, REACH * rows), jnp.float32),
+            pltpu.VMEM((HK, DH, (REACH + 1) * rows), keys.dtype),
+            pltpu.VMEM(((REACH + 1) * rows, DH), keys.dtype),
+            pltpu.VMEM((DH, 2 * rows), keys.dtype),
+            pltpu.VMEM((4, window, WIDTH), jnp.float32),
             dma((HK, 2)),
             dma((HK,)),
             dma((HK,)),

time: 87.2 us -> 50 us (0.57)
  Pallas kernels: 83.9 us -> 46.7 us
    pallas_call x1, Pallas kernels: 83.9 us -> 46.7 us  [on_device(): pl.pallas_call(functools.partial(kernel, shards), out_shape=jax.ShapeDtyp...]
where the time goes in v1:
time: 50 us; the launch traced here: 49.8 us
  Pallas kernels  46.7 us (93%)
  local copies, waits for them, and re-layouts  3.16 us (6%)
    pallas_call x1, Pallas kernels, on_device(): pl.pallas_call(functools.partial(kernel, shards), out_shape=jax.ShapeDtyp...  46.7 us
    unnamed x1, local copies, waits for them, and re-layouts  3.16 us

profile of v1, /device:TPU:15, one launch (start us, length us, event | category | flops | bytes accessed | tf_op | source)
XLA Modules:
  0.0 49.8 jit_solution(14245712476718902953)
XLA Ops:
  0.0 46.7 %shard_map.46 = bf16[512,2048]{1,0:T(8,128)(2,1)} custom-call(s32[256]{0:T(256)} %lengths_ref.1, bf16[512,2048]{1,0:T(8,128)(2,1)} %queries_ref.1, bf16[512,1024]{1,0:T(8,128)(2,1)} %keys_ref.1, bf16[512,1024]{1,0:T(8,128)(2,1)} %values_ref.1), custom_call_target="tpu_custom_call" | custom-call | tf_op jit(solution)/shard_map/pallas_call | solution.py:520
  46.7 3.2 %copy.6 = bf16[512,2048]{1,0:T(8,128)(2,1)} copy(bf16[512,2048]{1,0:T(8,128)(2,1)} %shard_map.46) | data formatting | bytes 4194304

commit v2 on v1

--- a/solution.py
+++ b/solution.py
@@ -48,6 +48,8 @@
     key_marks,
     query_marks,
     scores,
+    kept_mix,
+    kept_stat,
     load_sem,
     query_sem,
     out_sem,
@@ -57,6 +59,8 @@
     query_recv,
     slot_send,
     slot_recv,
+    first_send,
+    first_recv,
     relay_send,
     relay_recv,
     stat_send,
@@ -127,6 +131,19 @@
             me + 2,
         )
 
+    def first_older(side):
+        head = side * SPLIT
+        return remote(
+            held.at[head, :, own], held.at[head, :, far], first_send.at[side], first_recv.at[side], me + 2
+        )
+
+    def first_newer(side):
+        head = side * SPLIT
+        region = far if side else near
+        return remote(
+            held.at[head, :, own], held.at[head, :, region], first_send.at[side], slot_recv.at[0], me + 1 + side
+        )
+
     def relay(step, source, target):
         head = core * SPLIT + step
         return remote(
@@ -138,15 +155,23 @@
             stat_out.at[step], stat_in.at[head], stat_send.at[step], stat_recv.at[head], me + 2 - core
         )
 
-    @pl.loop(0, SPLIT)
+    for side in range(2):
+        for copy in loads(side * SPLIT):
+            copy.start()
+
+    @pl.loop(1, SPLIT)
     def _(step):
         query_load(step).start()
         query_load(SPLIT + step).start()
 
-    @pl.loop(0, HK)
-    def _(head):
-        for copy in loads(head):
-            copy.start()
+    @pl.loop(1, SPLIT)
+    def _(step):
+        for side in range(2):
+            for copy in loads(side * SPLIT + step):
+                copy.start()
+
+    query_load(0).start()
+    query_load(SPLIT).start()
 
     barrier = pltpu.get_barrier_semaphore()
 
@@ -175,7 +200,19 @@
     next_peers = jnp.where(has_next, 1 + core, 0)
     pl.semaphore_wait(barrier, 1 + back_peers + next_peers)
 
-    @pl.loop(0, SPLIT)
+    for side in range(2):
+        for copy in loads(side * SPLIT):
+            copy.wait()
+
+        @pl.when(jnp.logical_and(even, has_next))
+        def _():
+            first_older(side).start()
+
+        @pl.when(jnp.logical_and(odd, has_next))
+        def _():
+            first_newer(side).start()
+
+    @pl.loop(1, SPLIT)
     def _(step):
         for side in range(2):
             query_load(side * SPLIT + step).wait()
@@ -184,43 +221,56 @@
             def _():
                 query_to_prev(step, side).start()
 
-    @pl.loop(0, HK)
-    def _(head):
-        for copy in loads(head):
-            copy.wait()
-
-        @pl.when(even)
-        def _():
-            to_core(head, near).start()
-
-        @pl.when(jnp.logical_and(odd, head < SPLIT))
-        def _():
-            to_core(head, far).start()
+    @pl.when(even)
+    def _():
+        to_core(0, near).start()
+        to_core(SPLIT, near).start()
+
+    @pl.loop(1, SPLIT)
+    def _(step):
+        for side in range(2):
+            head = side * SPLIT + step
+            for copy in loads(head):
+                copy.wait()
+
+            @pl.when(even)
+            def _():
+                to_core(head, near).start()
+
+            if side == 0:
+
+                @pl.when(odd)
+                def _():
+                    to_core(head, far).start()
+
+    query_load(0).wait()
+    query_load(SPLIT).wait()
 
     @pl.when(jnp.logical_not(has_prev))
     def _():
         @pl.when(even)
         def _():
             held[:, :, near, :] = jnp.zeros((HK, 2, rows, DH), held.dtype)
+            for side in range(2):
+                held[side * SPLIT, :, far, :] = jnp.zeros((2, rows, DH), held.dtype)
             stat_in[...] = jnp.full(stat_in.shape, MASKED, jnp.float32)
 
         @pl.when(odd)
         def _():
             held[:, :, far, :] = jnp.zeros((HK, 2, rows, DH), held.dtype)
 
-    row = lax.broadcasted_iota(jnp.int32, (4 * tiles, TILE), 0)
-    lane = lax.broadcasted_iota(jnp.int32, (4 * tiles, TILE), 1)
-    far_begin = jnp.where(even, me + 1, me - 2) * rows
-    region_begin = jnp.where(
+    row = lax.broadcasted_iota(jnp.int32, (6 * tiles, TILE), 0)
+    lane = lax.broadcasted_iota(jnp.int32, (6 * tiles, TILE), 1)
+    begins_at = jnp.where(
         row < tiles,
-        far_begin,
+        jnp.where(even, me + 1, me - 2) * rows,
         jnp.where(
-            row < 2 * tiles,
-            (me - 1) * rows - rows,
-            jnp.where(row < 3 * tiles, me * rows - 2 * rows, next_begin - 3 * rows),
+            row < 3 * tiles,
+            (me - 2) * rows,
+            jnp.where(row < 4 * tiles, next_begin - 3 * rows, (me - 6) * rows),
         ),
     )
-    positions = region_begin + row * TILE + lane
+    positions = begins_at + row * TILE + lane
     edge_row = lax.broadcasted_iota(jnp.int32, (8, TILE), 0)
     edges = jnp.where(edge_row == 0, chip_begin, next_begin)
 
@@ -254,9 +304,15 @@
     def matches(block):
         return (feature == code_low[block : block + 1, :]) | (feature == code_high[block : block + 1, :])
 
-    for block in range(3 * tiles):
-        missing = jnp.where(matches(block), 0.0, -APART).astype(jnp.bfloat16)
-        key_marks[pl.ds(block * TILE, TILE), :] = missing.T
+    def mark(block):
+        return jnp.where(matches(block), 0.0, -APART).astype(jnp.bfloat16).T
+
+    for block in range(2 * tiles):
+        key_marks[0, pl.ds(block * TILE, TILE), :] = mark(block)
+        key_marks[1, pl.ds(block * TILE, TILE), :] = mark(4 * tiles + block)
+    for block in range(2 * tiles, 3 * tiles):
+        for kind in range(2):
+            key_marks[kind, pl.ds(block * TILE, TILE), :] = mark(block)
     for block in range(2 * tiles):
         present = jnp.where(matches(2 * tiles + block), 1.0, 0.0).astype(jnp.bfloat16)
         query_marks[:, pl.ds(block * TILE, TILE)] = present
@@ -281,7 +337,7 @@
         return cut
 
     def score_job(job, buffer):
-        head, queries, marks, spans, own_end, _ = job
+        head, queries, marks, kind, spans, own_end, _ = job
         state = {"highest": None, "buffer": buffer}
         turned_queries = jnp.concatenate([queries[:, g * DH : (g + 1) * DH].T for g in range(GROUPS)], axis=1)
         right = jnp.concatenate([turned_queries, jnp.concatenate([marks] * GROUPS, axis=1)], axis=0)
@@ -289,7 +345,7 @@
 
         def piece(begin, at, count):
             span = pl.ds(begin, count)
-            left = jnp.concatenate([held[head, 0, span, :], key_marks[span, :]], axis=1)
+            left = jnp.concatenate([held[head, 0, span, :], key_marks[kind, span, :]], axis=1)
             part = jnp.dot(left, right, preferred_element_type=jnp.float32)
             if own_end and at + count == total:
                 last = jnp.where(causal, part[count - TILE :], -APART)
@@ -304,7 +360,7 @@
         return state, [functools.partial(piece, *cut) for cut in pieces(spans, SCORE_KEYS)], finish
 
     def mix_job(job, state):
-        head, _, _, spans, _, store = job
+        head, _, _, _, spans, _, store = job
         buffer, highest = state["buffer"], state["row"]
         sums = {"totals": None, "mixed": None}
 
@@ -366,59 +422,97 @@
 
             spans = [(older + tile * TILE, rows - tile * TILE), (newer, rows)]
             marks = query_marks[:, pl.ds(rows + tile * TILE, TILE)]
-            jobs.append((head, query_back[step, span, :], marks, spans, False, store))
+            jobs.append((head, query_back[step, span, :], marks, 0, spans, False, store))
         run(jobs)
 
     def put(head, span, mixed):
         for g in range(GROUPS):
             out_held[head, span, pl.ds(g * DH, DH)] = mixed[:, g * DH : (g + 1) * DH].T
 
-    def attend_even(head):
+    def normal(head):
+        def store(tile, level, totals, mixed):
+            put(head, pl.ds(tile * TILE, TILE), (mixed * (1.0 / totals)).astype(jnp.bfloat16))
+
+        return store
+
+    def keep(side):
+        def store(tile, level, totals, mixed):
+            kept_mix[side, tile] = mixed
+            kept_stat[side, pl.ds(2 * tile, 1), :] = level
+            kept_stat[side, pl.ds(2 * tile + 1, 1), :] = totals
+
+        return store
+
+    def merged(head, side, partials):
+        def store(tile, level, totals, mixed):
+            span = pl.ds(tile * TILE, TILE)
+            top = level
+            if side is not None:
+                local = kept_stat[side, pl.ds(2 * tile, 1), :]
+                top = jnp.maximum(top, local)
+            if partials:
+                other = jnp.concatenate(
+                    [stat_in[head, pl.ds(tile * GROUPS + g, 1), :] for g in range(GROUPS)], axis=1
+                )
+                top = jnp.maximum(top, other)
+            here = jnp.exp2(level - top)
+            share = totals * here
+            if side is not None:
+                home = jnp.exp2(local - top)
+                share = share + kept_stat[side, pl.ds(2 * tile + 1, 1), :] * home
+            if partials:
+                there = jnp.exp2(other - top)
+                share = share + there
+            share = 1.0 / share
+            both = mixed * (here * share)
+            if side is not None:
+                both = both + kept_mix[side, tile] * (home * share)
+            if partials:
+                sent = pl.ds(rows + tile * TILE, TILE)
+                partial = jnp.concatenate([held[head, 0, sent, :].T, turned[head, :, sent]], axis=1)
+                both = both + partial.astype(jnp.float32) * (there * share)
+            put(head, span, both.astype(jnp.bfloat16))
+
+        return store
+
+    def jobs_of(head, kind, begin_of, end_of, own_end, store):
         jobs = []
         for tile in range(tiles):
             span = pl.ds(tile * TILE, TILE)
-
-            def store(level, totals, mixed, tile=tile, span=span):
-                sent = pl.ds(rows + tile * TILE, TILE)
-                other = jnp.concatenate(
-                    [stat_in[head, pl.ds(tile * GROUPS + g, 1), :] for g in range(GROUPS)], axis=1
-                )
-                top = jnp.maximum(level, other)
-                here = jnp.exp2(level - top)
-                there = jnp.exp2(other - top)
-                share = 1.0 / (totals * here + there)
-                partial = jnp.concatenate([held[head, 0, sent, :].T, turned[head, :, sent]], axis=1)
-                both = mixed * (here * share) + partial.astype(jnp.float32) * (there * share)
-                put(head, span, both.astype(jnp.bfloat16))
-
-            spans = [(rows, rows + (tile + 1) * TILE)]
-            marks = query_marks[:, span]
-            jobs.append((head, query_held[head, span, :], marks, spans, True, store))
-        run(jobs)
-
-    def attend_odd(head):
-        jobs = []
-        for tile in range(tiles):
-            span = pl.ds(tile * TILE, TILE)
-
-            def store(level, totals, mixed, span=span):
-                put(head, span, (mixed * (1.0 / totals)).astype(jnp.bfloat16))
-
-            spans = [(tile * TILE, REACH * rows + TILE)]
-            marks = query_marks[:, span]
-            jobs.append((head, query_held[head, span, :], marks, spans, True, store))
-        run(jobs)
+            spans = [(begin_of(tile), end_of(tile) - begin_of(tile))]
+            end = functools.partial(store, tile)
+            jobs.append((head, query_held[head, span, :], query_marks[:, span], kind, spans, own_end, end))
+        return jobs
+
+    def at_tile(tile):
+        return tile * TILE
+
+    def at_near(tile):
+        return rows
+
+    def at_own(tile):
+        return 2 * rows
+
+    def past_own(tile):
+        return 2 * rows + (tile + 1) * TILE
+
+    last = SPLIT - 1
 
     @pl.loop(0, HK)
     def _(head):
-        turn_values(head, REACH * rows)
+        turn_values(head, 2 * rows)
 
     @pl.when(even)
     def _():
-        @pl.loop(0, SPLIT)
-        def _(head):
-            to_core(head, far).wait_recv()
-            turn_values(head, 0)
+        jobs = []
+        for side in range(2):
+            jobs += jobs_of(side * SPLIT + last, 0, at_own, past_own, True, keep(side))
+        run(jobs)
+
+        @pl.loop(1, SPLIT)
+        def _(step):
+            to_core(step, far).wait_recv()
+            turn_values(step, 0)
 
     @pl.when(odd)
     def _():
@@ -427,9 +521,14 @@
             to_core(head, near).wait_recv()
             turn_values(head, rows)
 
-    @pl.loop(0, SPLIT + 1)
+        jobs = []
+        for side in range(2):
+            jobs += jobs_of(side * SPLIT + last, 0, at_near, past_own, True, keep(side))
+        run(jobs)
+
+    @pl.loop(1, SPLIT + 2)
     def _(turn):
-        @pl.when(jnp.logical_and(has_next, turn < SPLIT))
+        @pl.when(has_next & (turn < SPLIT))
         def _():
             query_to_prev(turn, 0).wait_recv()
 
@@ -445,9 +544,9 @@
 
             stat_to_next(turn, core * SPLIT + turn).start()
 
-        @pl.when(turn >= 1)
-        def _():
-            step = turn - 1
+        @pl.when(turn >= 2)
+        def _():
+            step = turn - 2
 
             @pl.when(has_prev)
             def _():
@@ -472,17 +571,45 @@
 
                 @pl.when(even)
                 def _():
-                    @pl.when(has_prev)
+                    turn_values(head, rows)
+
+                    @pl.when(step == 0)
+                    def _():
+                        @pl.when(jnp.logical_and(has_prev, turn_side == 0))
+                        def _():
+                            first_older(0).wait_recv()
+
+                        @pl.when(jnp.logical_and(has_prev, turn_side == 1))
+                        def _():
+                            first_older(1).wait_recv()
+
+                        turn_values(head, 0)
+                        run(jobs_of(head, 1, at_tile, past_own, True, normal(head)))
+
+                    @pl.when(jnp.logical_and(has_prev, step >= 1))
                     def _():
                         stat_to_next(step, head).wait_recv()
 
-                    turn_values(head, rows)
-                    attend_even(head)
+                    @pl.when(jnp.logical_and(step >= 1, step < last))
+                    def _():
+                        run(jobs_of(head, 0, at_near, past_own, True, merged(head, None, True)))
+
+                    @pl.when(step == last)
+                    def _():
+                        run(jobs_of(head, 0, at_near, at_own, False, merged(head, side, True)))
 
                 @pl.when(odd)
                 def _():
                     turn_values(head, 0)
-                    attend_odd(head)
+
+                    @pl.when(step < last)
+                    def _():
+                        kind = jnp.where(step == 0, 1, 0)
+                        run(jobs_of(head, kind, at_tile, past_own, True, normal(head)))
+
+                    @pl.when(step == last)
+                    def _():
+                        run(jobs_of(head, 0, at_tile, at_near, False, merged(head, side, False)))
 
                 out_store(head).start()
 
@@ -490,22 +617,33 @@
     def _(head):
         out_store(head).wait()
 
-        @pl.when(jnp.logical_or(even, head < SPLIT))
+        @pl.when(even)
         def _():
             to_core(head, near).wait_send()
+
+    @pl.when(has_next)
+    def _():
+        for side in range(2):
+            first_older(side).wait_send()
 
     @pl.loop(0, SPLIT)
     def _(step):
-        @pl.when(has_next)
-        def _():
-            slot_to_next(step, near).wait_send()
-            stat_to_next(step, step).wait_send()
-
         @pl.when(has_prev)
         def _():
             relay(step, near, far).wait_send()
 
-            @pl.when(even)
+        @pl.when(step >= 1)
+        def _():
+            @pl.when(odd)
+            def _():
+                to_core(step, far).wait_send()
+
+            @pl.when(has_next)
+            def _():
+                slot_to_next(step, near).wait_send()
+                stat_to_next(step, step).wait_send()
+
+            @pl.when(jnp.logical_and(even, has_prev))
             def _():
                 for side in range(2):
                     query_to_prev(step, side).wait_send()
@@ -536,9 +674,11 @@
             pltpu.VMEM((SPLIT, stats, TILE), jnp.float32),
             pltpu.VMEM((HK, stats, TILE), jnp.float32),
             pltpu.VMEM((HK, DH, (REACH + 1) * rows), keys.dtype),
-            pltpu.VMEM(((REACH + 1) * rows, DH), keys.dtype),
+            pltpu.VMEM((2, (REACH + 1) * rows, DH), keys.dtype),
             pltpu.VMEM((DH, 2 * rows), keys.dtype),
             pltpu.VMEM((4, window, WIDTH), jnp.float32),
+            pltpu.VMEM((2, rows // TILE, DH, WIDTH), jnp.float32),
+            pltpu.VMEM((2, 2 * (rows // TILE), WIDTH), jnp.float32),
             dma((HK, 2)),
             dma((HK,)),
             dma((HK,)),
@@ -548,6 +688,8 @@
             dma((SPLIT,)),
             dma((SPLIT,)),
             dma((SPLIT,)),
+            dma((2,)),
+            dma((2,)),
             dma((SPLIT,)),
             dma((SPLIT,)),
             dma((SPLIT,)),

time: 50 us -> 43.8 us (0.88)
  Pallas kernels: 46.7 us -> 40.5 us
    pallas_call x1, Pallas kernels: 46.7 us -> 40.5 us  [on_device(): pl.pallas_call(functools.partial(kernel, shards), out_shape=jax.ShapeDtyp...]
where the time goes in v2:
time: 43.8 us; the launch traced here: 43.6 us
  Pallas kernels  40.5 us (92%)
  local copies, waits for them, and re-layouts  3.16 us (7%)
    pallas_call x1, Pallas kernels, on_device(): pl.pallas_call(functools.partial(kernel, shards), out_shape=jax.ShapeDtyp...  40.5 us
    unnamed x1, local copies, waits for them, and re-layouts  3.16 us

profile of v2, /device:TPU:15, one launch (start us, length us, event | category | flops | bytes accessed | tf_op | source)
XLA Modules:
  0.0 43.6 jit_solution(12818233177490010617)
XLA Ops:
  0.0 40.5 %shard_map.46 = bf16[512,2048]{1,0:T(8,128)(2,1)} custom-call(s32[256]{0:T(256)} %lengths_ref.1, bf16[512,2048]{1,0:T(8,128)(2,1)} %queries_ref.1, bf16[512,1024]{1,0:T(8,128)(2,1)} %keys_ref.1, bf16[512,1024]{1,0:T(8,128)(2,1)} %values_ref.1), custom_call_target="tpu_custom_call" | custom-call | tf_op jit(solution)/shard_map/pallas_call | solution.py:658
  40.5 3.2 %copy.6 = bf16[512,2048]{1,0:T(8,128)(2,1)} copy(bf16[512,2048]{1,0:T(8,128)(2,1)} %shard_map.46) | data formatting | bytes 4194304

commit v3 on v2

--- a/solution.py
+++ b/solution.py
@@ -39,7 +39,6 @@
     out_ref,
     held,
     query_held,
-    out_held,
     query_back,
     slot,
     stat_out,
@@ -52,7 +51,6 @@
     kept_stat,
     load_sem,
     query_sem,
-    out_sem,
     core_send,
     core_recv,
     query_send,
@@ -65,6 +63,7 @@
     relay_recv,
     stat_send,
     stat_recv,
+    ready,
 ):
     me = lax.axis_index("cp")
     core = lax.rem(me, 2)
@@ -94,10 +93,6 @@
         lanes = pl.ds(pl.multiple_of(head * WIDTH, WIDTH), WIDTH)
         return pltpu.make_async_copy(queries_ref.at[:, lanes], query_held.at[head], query_sem.at[head])
 
-    def out_store(head):
-        lanes = pl.ds(pl.multiple_of(head * WIDTH, WIDTH), WIDTH)
-        return pltpu.make_async_copy(out_held.at[head], out_ref.at[:, lanes], out_sem.at[head])
-
     def remote(source, target, send, recv, device):
         return pltpu.make_async_remote_copy(
             src_ref=source,
@@ -131,18 +126,11 @@
             me + 2,
         )
 
-    def first_older(side):
-        head = side * SPLIT
-        return remote(
-            held.at[head, :, own], held.at[head, :, far], first_send.at[side], first_recv.at[side], me + 2
-        )
-
-    def first_newer(side):
-        head = side * SPLIT
-        region = far if side else near
-        return remote(
-            held.at[head, :, own], held.at[head, :, region], first_send.at[side], slot_recv.at[0], me + 1 + side
-        )
+    def first_older():
+        return remote(held.at[0, :, own], held.at[0, :, far], first_send, first_recv, me + 2)
+
+    def first_newer():
+        return remote(held.at[0, :, own], held.at[0, :, near], first_send, slot_recv.at[0], me + 1)
 
     def relay(step, source, target):
         head = core * SPLIT + step
@@ -155,23 +143,21 @@
             stat_out.at[step], stat_in.at[head], stat_send.at[step], stat_recv.at[head], me + 2 - core
         )
 
-    for side in range(2):
-        for copy in loads(side * SPLIT):
-            copy.start()
+    for copy in loads(0):
+        copy.start()
+    query_load(SPLIT).start()
 
     @pl.loop(1, SPLIT)
     def _(step):
         query_load(step).start()
         query_load(SPLIT + step).start()
 
-    @pl.loop(1, SPLIT)
-    def _(step):
-        for side in range(2):
-            for copy in loads(side * SPLIT + step):
-                copy.start()
+    @pl.loop(1, HK)
+    def _(head):
+        for copy in loads(head):
+            copy.start()
 
     query_load(0).start()
-    query_load(SPLIT).start()
 
     barrier = pltpu.get_barrier_semaphore()
 
@@ -188,29 +174,33 @@
         def _():
             greet(me - 1)
 
+    next_peers = jnp.where(has_next, 1 + core, 0)
+    pl.semaphore_wait(barrier, 1 + next_peers)
+
     @pl.when(has_next)
     def _():
-        greet(me + 2)
-
-        @pl.when(odd)
-        def _():
-            greet(me + 1)
-
-    back_peers = jnp.where(has_prev, 2 - core, 0)
-    next_peers = jnp.where(has_next, 1 + core, 0)
-    pl.semaphore_wait(barrier, 1 + back_peers + next_peers)
-
-    for side in range(2):
-        for copy in loads(side * SPLIT):
-            copy.wait()
-
-        @pl.when(jnp.logical_and(even, has_next))
-        def _():
-            first_older(side).start()
-
-        @pl.when(jnp.logical_and(odd, has_next))
-        def _():
-            first_newer(side).start()
+        pl.semaphore_signal(ready, inc=1, device_id={"cp": me + 2 - core}, device_id_type=MESH)
+
+    for copy in loads(0):
+        copy.wait()
+
+    @pl.when(jnp.logical_and(even, has_next))
+    def _():
+        first_older().start()
+
+    @pl.when(jnp.logical_and(odd, has_next))
+    def _():
+        first_newer().start()
+
+    @pl.when(jnp.logical_and(even, has_prev))
+    def _():
+        pl.semaphore_wait(ready, 2)
+
+    query_load(SPLIT).wait()
+
+    @pl.when(jnp.logical_and(even, has_prev))
+    def _():
+        query_to_prev(0, 1).start()
 
     @pl.loop(1, SPLIT)
     def _(step):
@@ -224,35 +214,28 @@
     @pl.when(even)
     def _():
         to_core(0, near).start()
-        to_core(SPLIT, near).start()
-
-    @pl.loop(1, SPLIT)
-    def _(step):
-        for side in range(2):
-            head = side * SPLIT + step
-            for copy in loads(head):
-                copy.wait()
-
-            @pl.when(even)
-            def _():
-                to_core(head, near).start()
-
-            if side == 0:
-
-                @pl.when(odd)
-                def _():
-                    to_core(head, far).start()
+
+    @pl.loop(1, HK)
+    def _(head):
+        for copy in loads(head):
+            copy.wait()
+
+        @pl.when(even)
+        def _():
+            to_core(head, near).start()
+
+        @pl.when(jnp.logical_and(odd, head < SPLIT))
+        def _():
+            to_core(head, far).start()
 
     query_load(0).wait()
-    query_load(SPLIT).wait()
 
     @pl.when(jnp.logical_not(has_prev))
     def _():
         @pl.when(even)
         def _():
             held[:, :, near, :] = jnp.zeros((HK, 2, rows, DH), held.dtype)
-            for side in range(2):
-                held[side * SPLIT, :, far, :] = jnp.zeros((2, rows, DH), held.dtype)
+            held[0, :, far, :] = jnp.zeros((2, rows, DH), held.dtype)
             stat_in[...] = jnp.full(stat_in.shape, MASKED, jnp.float32)
 
         @pl.when(odd)
@@ -427,7 +410,8 @@
 
     def put(head, span, mixed):
         for g in range(GROUPS):
-            out_held[head, span, pl.ds(g * DH, DH)] = mixed[:, g * DH : (g + 1) * DH].T
+            lanes = pl.ds(pl.multiple_of(head * WIDTH + g * DH, DH), DH)
+            out_ref[span, lanes] = mixed[:, g * DH : (g + 1) * DH].T
 
     def normal(head):
         def store(tile, level, totals, mixed):
@@ -526,23 +510,21 @@
             jobs += jobs_of(side * SPLIT + last, 0, at_near, past_own, True, keep(side))
         run(jobs)
 
-    @pl.loop(1, SPLIT + 2)
+    @pl.loop(0, SPLIT + 2)
     def _(turn):
-        @pl.when(has_next & (turn < SPLIT))
+        @pl.when(has_next & even & (turn >= 1) & (turn < SPLIT))
         def _():
             query_to_prev(turn, 0).wait_recv()
-
-            @pl.when(even)
-            def _():
-                attend_back(turn, turn, 2 * rows, 0)
-                slot_to_next(turn, near).start()
-
-            @pl.when(odd)
-            def _():
-                attend_back(SPLIT + turn, turn, rows, 2 * rows)
-                slot_to_next(turn, far).start()
-
-            stat_to_next(turn, core * SPLIT + turn).start()
+            attend_back(turn, turn, 2 * rows, 0)
+            slot_to_next(turn, near).start()
+            stat_to_next(turn, turn).start()
+
+        @pl.when(has_next & odd & (turn < SPLIT))
+        def _():
+            query_to_prev(turn, 1).wait_recv()
+            attend_back(SPLIT + turn, turn, rows, 2 * rows)
+            slot_to_next(turn, far).start()
+            stat_to_next(turn, SPLIT + turn).start()
 
         @pl.when(turn >= 2)
         def _():
@@ -573,24 +555,20 @@
                 def _():
                     turn_values(head, rows)
 
-                    @pl.when(step == 0)
+                    @pl.when(head == 0)
                     def _():
-                        @pl.when(jnp.logical_and(has_prev, turn_side == 0))
+                        @pl.when(has_prev)
                         def _():
-                            first_older(0).wait_recv()
-
-                        @pl.when(jnp.logical_and(has_prev, turn_side == 1))
-                        def _():
-                            first_older(1).wait_recv()
-
-                        turn_values(head, 0)
-                        run(jobs_of(head, 1, at_tile, past_own, True, normal(head)))
-
-                    @pl.when(jnp.logical_and(has_prev, step >= 1))
+                            first_older().wait_recv()
+
+                        turn_values(0, 0)
+                        run(jobs_of(0, 1, at_tile, past_own, True, normal(0)))
+
+                    @pl.when(jnp.logical_and(has_prev, head >= 1))
                     def _():
                         stat_to_next(step, head).wait_recv()
 
-                    @pl.when(jnp.logical_and(step >= 1, step < last))
+                    @pl.when(jnp.logical_and(head >= 1, step < last))
                     def _():
                         run(jobs_of(head, 0, at_near, past_own, True, merged(head, None, True)))
 
@@ -604,47 +582,51 @@
 
                     @pl.when(step < last)
                     def _():
-                        kind = jnp.where(step == 0, 1, 0)
+                        kind = jnp.where(head == 0, 1, 0)
                         run(jobs_of(head, kind, at_tile, past_own, True, normal(head)))
 
                     @pl.when(step == last)
                     def _():
                         run(jobs_of(head, 0, at_tile, at_near, False, merged(head, side, False)))
 
-                out_store(head).start()
-
-    @pl.loop(0, HK)
-    def _(head):
-        out_store(head).wait()
+    @pl.when(even)
+    def _():
+        @pl.loop(0, HK)
+        def _(head):
+            to_core(head, near).wait_send()
+
+    @pl.when(odd)
+    def _():
+        @pl.loop(1, SPLIT)
+        def _(head):
+            to_core(head, far).wait_send()
+
+    @pl.when(has_next)
+    def _():
+        first_older().wait_send()
+
+        @pl.when(odd)
+        def _():
+            slot_to_next(0, far).wait_send()
+            stat_to_next(0, SPLIT).wait_send()
+
+        @pl.loop(1, SPLIT)
+        def _(step):
+            slot_to_next(step, near).wait_send()
+            stat_to_next(step, step).wait_send()
+
+    @pl.when(has_prev)
+    def _():
+        @pl.loop(0, SPLIT)
+        def _(step):
+            relay(step, near, far).wait_send()
 
         @pl.when(even)
         def _():
-            to_core(head, near).wait_send()
-
-    @pl.when(has_next)
-    def _():
-        for side in range(2):
-            first_older(side).wait_send()
-
-    @pl.loop(0, SPLIT)
-    def _(step):
-        @pl.when(has_prev)
-        def _():
-            relay(step, near, far).wait_send()
-
-        @pl.when(step >= 1)
-        def _():
-            @pl.when(odd)
-            def _():
-                to_core(step, far).wait_send()
-
-            @pl.when(has_next)
-            def _():
-                slot_to_next(step, near).wait_send()
-                stat_to_next(step, step).wait_send()
-
-            @pl.when(jnp.logical_and(even, has_prev))
-            def _():
+            query_to_prev(0, 1).wait_send()
+
+            @pl.loop(1, SPLIT)
+            def _(step):
                 for side in range(2):
                     query_to_prev(step, side).wait_send()
 
@@ -657,17 +639,16 @@
     dma = pltpu.SemaphoreType.DMA
     return pl.pallas_call(
         functools.partial(kernel, shards),
-        out_shape=jax.ShapeDtypeStruct(queries.shape, queries.dtype),
+        out_shape=pltpu.VMEM(queries.shape, queries.dtype),
         in_specs=[
             pl.BlockSpec(memory_space=pltpu.SMEM),
             pl.BlockSpec(memory_space=pl.ANY),
             pl.BlockSpec(memory_space=pl.ANY),
             pl.BlockSpec(memory_space=pl.ANY),
         ],
-        out_specs=pl.BlockSpec(memory_space=pl.ANY),
+        out_specs=pl.BlockSpec(memory_space=pltpu.VMEM),
         scratch_shapes=[
             pltpu.VMEM((HK, 2, (REACH + 1) * rows, DH), keys.dtype),
-            pltpu.VMEM((HK, rows, WIDTH), queries.dtype),
             pltpu.VMEM((HK, rows, WIDTH), queries.dtype),
             pltpu.VMEM((SPLIT, rows, WIDTH), queries.dtype),
             pltpu.VMEM((SPLIT, 2, rows, DH), keys.dtype),
@@ -684,21 +665,21 @@
             dma((HK,)),
             dma((HK,)),
             dma((HK,)),
-            dma((HK,)),
             dma((SPLIT,)),
             dma((SPLIT,)),
             dma((SPLIT,)),
-            dma((2,)),
-            dma((2,)),
+            dma(()),
+            dma(()),
             dma((SPLIT,)),
             dma((SPLIT,)),
             dma((SPLIT,)),
             dma((HK,)),
+            pltpu.SemaphoreType.REGULAR,
         ],
         compiler_params=pltpu.CompilerParams(
-            collective_id=0, has_side_effects=True, vmem_limit_bytes=58 * 1024 * 1024
+            collective_id=0, has_side_effects=True, vmem_limit_bytes=36 * 1024 * 1024
         ),
-    )(doc_lengths, queries, keys, values)
+    )(*(pltpu.with_memory_space_constraint(x, pltpu.HBM) for x in (doc_lengths, queries, keys, values)))
 
 
 def solution(mesh):

time: 43.8 us -> 43.6 us (level)
  local copies, waits for them, and re-layouts: 3.16 us -> 1.32 us
  Pallas kernels: 40.5 us -> 41.8 us
    unnamed x1, local copies, waits for them, and re-layouts: 3.16 us -> 1.32 us
    pallas_call x1, Pallas kernels: 40.5 us -> 41.8 us  [on_device(): pl.pallas_call(functools.partial(kernel, shards), out_shape=pltpu.VMEM(qu...]
where the time goes in v3:
time: 43.6 us; the launch traced here: 43.2 us
  Pallas kernels  41.8 us (96%)
  local copies, waits for them, and re-layouts  1.32 us (3%)
    pallas_call x1, Pallas kernels, on_device(): pl.pallas_call(functools.partial(kernel, shards), out_shape=pltpu.VMEM(qu...  41.8 us
    unnamed x1, local copies, waits for them, and re-layouts  1.32 us

profile of v3, /device:TPU:15, one launch (start us, length us, event | category | flops | bytes accessed | tf_op | source)
XLA Modules:
  0.0 43.2 jit_solution(8690249821797875590)
XLA Ops:
  0.0 41.8 %shard_map.46 = bf16[512,2048]{1,0:T(8,128)(2,1)S(1)} custom-call(s32[256]{0:T(256)} %lengths_ref.1, bf16[512,2048]{1,0:T(8,128)(2,1)} %queries_ref.1, bf16[512,1024]{1,0:T(8,128)(2,1)} %keys_ref.1, bf16[512,1024]{1,0:T(8,128)(2,1)} %values_ref.1), custom_call_target="tpu_custom_call" | custom-call | tf_op jit(solution)/shard_map/pallas_call | solution.py:640
  41.8 1.3 %copy.6 = bf16[512,2048]{1,0:T(8,128)(2,1)} copy(bf16[512,2048]{1,0:T(8,128)(2,1)S(1)} %shard_map.46) | data formatting | bytes 4194304

commit v4 on v2

--- a/solution.py
+++ b/solution.py
@@ -23,6 +23,7 @@
 LOG2E = math.log2(math.e)
 SPLIT = HK // 2
 MODULUS = 63
+PARTS = 2
 APART = 65536.0
 SCORE_KEYS = 640
 MIX_KEYS = 256
@@ -39,7 +40,6 @@
     out_ref,
     held,
     query_held,
-    out_held,
     query_back,
     slot,
     stat_out,
@@ -52,7 +52,6 @@
     kept_stat,
     load_sem,
     query_sem,
-    out_sem,
     core_send,
     core_recv,
     query_send,
@@ -65,6 +64,7 @@
     relay_recv,
     stat_send,
     stat_recv,
+    ready,
 ):
     me = lax.axis_index("cp")
     core = lax.rem(me, 2)
@@ -75,6 +75,7 @@
     docs = lengths_ref.shape[0]
     tiles = rows // TILE
     window = REACH * rows + TILE
+    piece_rows = rows // PARTS
     own = pl.ds(REACH * rows, rows)
     near = pl.ds(rows, rows)
     far = pl.ds(0, rows)
@@ -93,10 +94,6 @@
     def query_load(head):
         lanes = pl.ds(pl.multiple_of(head * WIDTH, WIDTH), WIDTH)
         return pltpu.make_async_copy(queries_ref.at[:, lanes], query_held.at[head], query_sem.at[head])
-
-    def out_store(head):
-        lanes = pl.ds(pl.multiple_of(head * WIDTH, WIDTH), WIDTH)
-        return pltpu.make_async_copy(out_held.at[head], out_ref.at[:, lanes], out_sem.at[head])
 
     def remote(source, target, send, recv, device):
         return pltpu.make_async_remote_copy(
@@ -113,21 +110,25 @@
             held.at[head, :, own], held.at[head, :, region], core_send.at[head], core_recv.at[head], partner
         )
 
-    def query_to_prev(step, side):
+    def part_of(region, part):
+        return pl.ds(region + part * piece_rows, piece_rows)
+
+    def query_to_prev(step, side, part):
+        head = side * SPLIT + step
         return remote(
-            query_held.at[side * SPLIT + step],
-            query_back.at[step],
-            query_send.at[side * SPLIT + step],
-            query_recv.at[step],
+            query_held.at[head, part_of(0, part)],
+            query_back.at[step, part_of(0, part)],
+            query_send.at[head, part],
+            query_recv.at[step, part],
             me - 2 + side,
         )
 
-    def slot_to_next(step, region):
+    def slot_to_next(step, region, part):
         return remote(
-            slot.at[step],
-            held.at[core * SPLIT + step, :, region],
-            slot_send.at[step],
-            slot_recv.at[step],
+            slot.at[step, :, part_of(0, part)],
+            held.at[core * SPLIT + step, :, part_of(region, part)],
+            slot_send.at[step, part],
+            slot_recv.at[step, part],
             me + 2,
         )
 
@@ -141,13 +142,21 @@
         head = side * SPLIT
         region = far if side else near
         return remote(
-            held.at[head, :, own], held.at[head, :, region], first_send.at[side], slot_recv.at[0], me + 1 + side
-        )
-
-    def relay(step, source, target):
+            held.at[head, :, own],
+            held.at[head, :, region],
+            first_send.at[side],
+            first_recv.at[2 + side],
+            me + 1 + side,
+        )
+
+    def relay(step, source, target, part):
         head = core * SPLIT + step
         return remote(
-            held.at[head, :, source], held.at[head, :, target], relay_send.at[step], relay_recv.at[step], partner
+            held.at[head, :, part_of(source, part)],
+            held.at[head, :, part_of(target, part)],
+            relay_send.at[step, part],
+            relay_recv.at[step, part],
+            partner,
         )
 
     def stat_to_next(step, head):
@@ -188,17 +197,12 @@
         def _():
             greet(me - 1)
 
+    next_peers = jnp.where(has_next, 1 + core, 0)
+    pl.semaphore_wait(barrier, 1 + next_peers)
+
     @pl.when(has_next)
     def _():
-        greet(me + 2)
-
-        @pl.when(odd)
-        def _():
-            greet(me + 1)
-
-    back_peers = jnp.where(has_prev, 2 - core, 0)
-    next_peers = jnp.where(has_next, 1 + core, 0)
-    pl.semaphore_wait(barrier, 1 + back_peers + next_peers)
+        pl.semaphore_signal(ready, inc=1, device_id={"cp": me + 2 - core}, device_id_type=MESH)
 
     for side in range(2):
         for copy in loads(side * SPLIT):
@@ -211,15 +215,6 @@
         @pl.when(jnp.logical_and(odd, has_next))
         def _():
             first_newer(side).start()
-
-    @pl.loop(1, SPLIT)
-    def _(step):
-        for side in range(2):
-            query_load(side * SPLIT + step).wait()
-
-            @pl.when(jnp.logical_and(even, has_prev))
-            def _():
-                query_to_prev(step, side).start()
 
     @pl.when(even)
     def _():
@@ -242,6 +237,20 @@
                 @pl.when(odd)
                 def _():
                     to_core(head, far).start()
+
+    @pl.when(jnp.logical_and(even, has_prev))
+    def _():
+        pl.semaphore_wait(ready, 2)
+
+    @pl.loop(1, SPLIT)
+    def _(step):
+        for side in range(2):
+            query_load(side * SPLIT + step).wait()
+
+            @pl.when(jnp.logical_and(even, has_prev))
+            def _():
+                for part in range(PARTS):
+                    query_to_prev(step, side, part).start()
 
     query_load(0).wait()
     query_load(SPLIT).wait()
@@ -357,7 +366,7 @@
         def finish():
             state["row"] = jnp.max(state["highest"], axis=0, keepdims=True)
 
-        return state, [functools.partial(piece, *cut) for cut in pieces(spans, SCORE_KEYS)], finish
+        return state, [functools.partial(piece, *cut) for cut in pieces(spans, SCORE_KEYS if own_end else 256)], finish
 
     def mix_job(job, state):
         head, _, _, _, spans, _, store = job
@@ -403,9 +412,9 @@
                 score_end()
             before = (job, state)
 
-    def attend_back(head, step, older, newer):
+    def attend_back(head, step, older, newer, part):
         jobs = []
-        for tile in range(tiles):
+        for tile in range(part * tiles // PARTS, (part + 1) * tiles // PARTS):
             span = pl.ds(tile * TILE, TILE)
 
             def store(level, totals, mixed, tile=tile, span=span):
@@ -427,7 +436,8 @@
 
     def put(head, span, mixed):
         for g in range(GROUPS):
-            out_held[head, span, pl.ds(g * DH, DH)] = mixed[:, g * DH : (g + 1) * DH].T
+            lanes = pl.ds(pl.multiple_of(head * WIDTH + g * DH, DH), DH)
+            out_ref[span, lanes] = mixed[:, g * DH : (g + 1) * DH].T
 
     def normal(head):
         def store(tile, level, totals, mixed):
@@ -496,7 +506,7 @@
     def past_own(tile):
         return 2 * rows + (tile + 1) * TILE
 
-    last = SPLIT - 1
+    early = SPLIT - 2
 
     @pl.loop(0, HK)
     def _(head):
@@ -504,11 +514,6 @@
 
     @pl.when(even)
     def _():
-        jobs = []
-        for side in range(2):
-            jobs += jobs_of(side * SPLIT + last, 0, at_own, past_own, True, keep(side))
-        run(jobs)
-
         @pl.loop(1, SPLIT)
         def _(step):
             to_core(step, far).wait_recv()
@@ -521,28 +526,37 @@
             to_core(head, near).wait_recv()
             turn_values(head, rows)
 
-        jobs = []
-        for side in range(2):
-            jobs += jobs_of(side * SPLIT + last, 0, at_near, past_own, True, keep(side))
-        run(jobs)
-
-    @pl.loop(1, SPLIT + 2)
-    def _(turn):
-        @pl.when(has_next & (turn < SPLIT))
-        def _():
-            query_to_prev(turn, 0).wait_recv()
-
-            @pl.when(even)
+    @pl.loop(0, SPLIT + 3)
+    def _(count):
+        turn = count - 1
+
+        @pl.when(has_next & even & (turn >= 1) & (turn < SPLIT))
+        def _():
+            for part in range(PARTS):
+                query_to_prev(turn, 0, part).wait_recv()
+                attend_back(turn, turn, 2 * rows, 0, part)
+                slot_to_next(turn, rows, part).start()
+
+            stat_to_next(turn, turn).start()
+
+        @pl.when(has_next & odd & (turn >= 1) & (turn < SPLIT))
+        def _():
+            for part in range(PARTS):
+                query_to_prev(turn, 1, part).wait_recv()
+                attend_back(SPLIT + turn, turn, rows, 2 * rows, part)
+                slot_to_next(turn, 0, part).start()
+
+            stat_to_next(turn, SPLIT + turn).start()
+
+        for which, begin in ((even, at_own), (odd, at_near)):
+
+            @pl.when(which & (turn <= 0))
             def _():
-                attend_back(turn, turn, 2 * rows, 0)
-                slot_to_next(turn, near).start()
-
-            @pl.when(odd)
-            def _():
-                attend_back(SPLIT + turn, turn, rows, 2 * rows)
-                slot_to_next(turn, far).start()
-
-            stat_to_next(turn, core * SPLIT + turn).start()
+                jobs = []
+                for side in range(2):
+                    head = side * SPLIT + early - turn
+                    jobs += jobs_of(head, 0, begin, past_own, True, keep(-2 * turn + side))
+                run(jobs)
 
         @pl.when(turn >= 2)
         def _():
@@ -550,15 +564,29 @@
 
             @pl.when(has_prev)
             def _():
-                slot_to_next(step, far).wait_recv()
-
-                @pl.when(even)
+                @pl.when(jnp.logical_and(even, step == 0))
                 def _():
-                    relay(step, near, far).start()
-
-                @pl.when(odd)
+                    first_newer(0).wait_recv()
+                    for part in range(PARTS):
+                        relay(step, rows, 0, part).start()
+
+                @pl.when(jnp.logical_and(odd, step == 0))
                 def _():
-                    relay(step, far, near).start()
+                    first_newer(1).wait_recv()
+                    for part in range(PARTS):
+                        relay(step, 0, rows, part).start()
+
+                @pl.when(jnp.logical_and(even, step >= 1))
+                def _():
+                    for part in range(PARTS):
+                        slot_to_next(step, rows, part).wait_recv()
+                        relay(step, rows, 0, part).start()
+
+                @pl.when(jnp.logical_and(odd, step >= 1))
+                def _():
+                    for part in range(PARTS):
+                        slot_to_next(step, 0, part).wait_recv()
+                        relay(step, 0, rows, part).start()
 
             @pl.loop(0, 2)
             def _(turn_side):
@@ -567,7 +595,8 @@
 
                 @pl.when(jnp.logical_and(has_prev, turn_side == 1))
                 def _():
-                    relay(step, near, far).wait_recv()
+                    for part in range(PARTS):
+                        relay(step, 0, rows, part).wait_recv()
 
                 @pl.when(even)
                 def _():
@@ -590,63 +619,64 @@
                     def _():
                         stat_to_next(step, head).wait_recv()
 
-                    @pl.when(jnp.logical_and(step >= 1, step < last))
+                    @pl.when(jnp.logical_and(step >= 1, step < early))
                     def _():
                         run(jobs_of(head, 0, at_near, past_own, True, merged(head, None, True)))
 
-                    @pl.when(step == last)
+                    @pl.when(step >= early)
                     def _():
-                        run(jobs_of(head, 0, at_near, at_own, False, merged(head, side, True)))
+                        run(jobs_of(head, 0, at_near, at_own, False, merged(head, 2 * (step - early) + side, True)))
 
                 @pl.when(odd)
                 def _():
                     turn_values(head, 0)
 
-                    @pl.when(step < last)
+                    @pl.when(step < early)
                     def _():
                         kind = jnp.where(step == 0, 1, 0)
                         run(jobs_of(head, kind, at_tile, past_own, True, normal(head)))
 
-                    @pl.when(step == last)
+                    @pl.when(step >= early)
                     def _():
-                        run(jobs_of(head, 0, at_tile, at_near, False, merged(head, side, False)))
-
-                out_store(head).start()
-
-    @pl.loop(0, HK)
-    def _(head):
-        out_store(head).wait()
-
-        @pl.when(even)
-        def _():
+                        run(jobs_of(head, 0, at_tile, at_near, False, merged(head, 2 * (step - early) + side, False)))
+
+    @pl.when(even)
+    def _():
+        @pl.loop(0, HK)
+        def _(head):
             to_core(head, near).wait_send()
+
+    @pl.when(odd)
+    def _():
+        @pl.loop(1, SPLIT)
+        def _(head):
+            to_core(head, far).wait_send()
 
     @pl.when(has_next)
     def _():
         for side in range(2):
             first_older(side).wait_send()
 
-    @pl.loop(0, SPLIT)
-    def _(step):
-        @pl.when(has_prev)
-        def _():
-            relay(step, near, far).wait_send()
-
-        @pl.when(step >= 1)
-        def _():
-            @pl.when(odd)
-            def _():
-                to_core(step, far).wait_send()
-
-            @pl.when(has_next)
-            def _():
-                slot_to_next(step, near).wait_send()
-                stat_to_next(step, step).wait_send()
-
-            @pl.when(jnp.logical_and(even, has_prev))
-            def _():
+        @pl.loop(1, SPLIT)
+        def _(step):
+            for part in range(PARTS):
+                slot_to_next(step, 0, part).wait_send()
+            stat_to_next(step, step).wait_send()
+
+    @pl.when(has_prev)
+    def _():
+        @pl.loop(0, SPLIT)
+        def _(step):
+            for part in range(PARTS):
+                relay(step, 0, rows, part).wait_send()
+
+        @pl.when(even)
+        def _():
+            @pl.loop(1, SPLIT)
+            def _(step):
                 for side in range(2):
-                    query_to_prev(step, side).wait_send()
+                    for part in range(PARTS):
+                        query_to_prev(step, side, part).wait_send()
 
 
 def on_device(queries, keys, values, doc_lengths):
@@ -657,17 +687,16 @@
     dma = pltpu.SemaphoreType.DMA
     return pl.pallas_call(
         functools.partial(kernel, shards),
-        out_shape=jax.ShapeDtypeStruct(queries.shape, queries.dtype),
+        out_shape=pltpu.VMEM(queries.shape, queries.dtype),
         in_specs=[
             pl.BlockSpec(memory_space=pltpu.SMEM),
             pl.BlockSpec(memory_space=pl.ANY),
             pl.BlockSpec(memory_space=pl.ANY),
             pl.BlockSpec(memory_space=pl.ANY),
         ],
-        out_specs=pl.BlockSpec(memory_space=pl.ANY),
+        out_specs=pl.BlockSpec(memory_space=pltpu.VMEM),
         scratch_shapes=[
             pltpu.VMEM((HK, 2, (REACH + 1) * rows, DH), keys.dtype),
-            pltpu.VMEM((HK, rows, WIDTH), queries.dtype),
             pltpu.VMEM((HK, rows, WIDTH), queries.dtype),
             pltpu.VMEM((SPLIT, rows, WIDTH), queries.dtype),
             pltpu.VMEM((SPLIT, 2, rows, DH), keys.dtype),
@@ -677,28 +706,28 @@
             pltpu.VMEM((2, (REACH + 1) * rows, DH), keys.dtype),
             pltpu.VMEM((DH, 2 * rows), keys.dtype),
             pltpu.VMEM((4, window, WIDTH), jnp.float32),
-            pltpu.VMEM((2, rows // TILE, DH, WIDTH), jnp.float32),
-            pltpu.VMEM((2, 2 * (rows // TILE), WIDTH), jnp.float32),
+            pltpu.VMEM((4, rows // TILE, DH, WIDTH), jnp.float32),
+            pltpu.VMEM((4, 2 * (rows // TILE), WIDTH), jnp.float32),
             dma((HK, 2)),
             dma((HK,)),
             dma((HK,)),
             dma((HK,)),
-            dma((HK,)),
-            dma((HK,)),
-            dma((SPLIT,)),
-            dma((SPLIT,)),
-            dma((SPLIT,)),
+            dma((HK, PARTS)),
+            dma((SPLIT, PARTS)),
+            dma((SPLIT, PARTS)),
+            dma((SPLIT, PARTS)),
             dma((2,)),
-            dma((2,)),
-            dma((SPLIT,)),
-            dma((SPLIT,)),
+            dma((4,)),
+            dma((SPLIT, PARTS)),
+            dma((SPLIT, PARTS)),
             dma((SPLIT,)),
             dma((HK,)),
+            pltpu.SemaphoreType.REGULAR,
         ],
         compiler_params=pltpu.CompilerParams(
-            collective_id=0, has_side_effects=True, vmem_limit_bytes=58 * 1024 * 1024
+            collective_id=0, has_side_effects=True, vmem_limit_bytes=36 * 1024 * 1024
         ),
-    )(doc_lengths, queries, keys, values)
+    )(*(pltpu.with_memory_space_constraint(x, pltpu.HBM) for x in (doc_lengths, queries, keys, values)))
 
 
 def solution(mesh):

time: 43.8 us -> 41.9 us (0.957)
  local copies, waits for them, and re-layouts: 3.16 us -> 1.32 us
    unnamed x1, local copies, waits for them, and re-layouts: 3.16 us -> 1.32 us
where the time goes in v4:
time: 41.9 us; the launch traced here: 41.6 us
  Pallas kernels  40.3 us (96%)
  local copies, waits for them, and re-layouts  1.32 us (3%)
    pallas_call x1, Pallas kernels, on_device(): pl.pallas_call(functools.partial(kernel, shards), out_shape=pltpu.VMEM(qu...  40.3 us
    unnamed x1, local copies, waits for them, and re-layouts  1.32 us

profile of v4, /device:TPU:15, one launch (start us, length us, event | category | flops | bytes accessed | tf_op | source)
XLA Modules:
  0.0 41.6 jit_solution(10716938186045157990)
XLA Ops:
  0.0 40.3 %shard_map.46 = bf16[512,2048]{1,0:T(8,128)(2,1)S(1)} custom-call(s32[256]{0:T(256)} %lengths_ref.1, bf16[512,2048]{1,0:T(8,128)(2,1)} %queries_ref.1, bf16[512,1024]{1,0:T(8,128)(2,1)} %keys_ref.1, bf16[512,1024]{1,0:T(8,128)(2,1)} %values_ref.1), custom_call_target="tpu_custom_call" | custom-call | tf_op jit(solution)/shard_map/pallas_call | solution.py:688
  40.3 1.3 %copy.6 = bf16[512,2048]{1,0:T(8,128)(2,1)} copy(bf16[512,2048]{1,0:T(8,128)(2,1)S(1)} %shard_map.46) | data formatting | bytes 4194304

commit v5 on v4

--- a/solution.py
+++ b/solution.py
@@ -23,7 +23,7 @@
 LOG2E = math.log2(math.e)
 SPLIT = HK // 2
 MODULUS = 63
-PARTS = 2
+PARTS = 1
 APART = 65536.0
 SCORE_KEYS = 640
 MIX_KEYS = 256

time: 41.9 us -> 41.2 us (0.983)
  Pallas kernels: 40.3 us -> 39.7 us
    pallas_call x1, Pallas kernels: 40.3 us -> 39.7 us  [on_device(): pl.pallas_call(functools.partial(kernel, shards), out_shape=pltpu.VMEM(qu...]
where the time goes in v5:
time: 41.2 us; the launch traced here: 41 us
  Pallas kernels  39.7 us (96%)
  local copies, waits for them, and re-layouts  1.32 us (3%)
    pallas_call x1, Pallas kernels, on_device(): pl.pallas_call(functools.partial(kernel, shards), out_shape=pltpu.VMEM(qu...  39.7 us
    unnamed x1, local copies, waits for them, and re-layouts  1.32 us

profile of v5, /device:TPU:15, one launch (start us, length us, event | category | flops | bytes accessed | tf_op | source)
XLA Modules:
  0.0 41.0 jit_solution(9942980656045371904)
XLA Ops:
  0.0 39.7 %shard_map.46 = bf16[512,2048]{1,0:T(8,128)(2,1)S(1)} custom-call(s32[256]{0:T(256)} %lengths_ref.1, bf16[512,2048]{1,0:T(8,128)(2,1)} %queries_ref.1, bf16[512,1024]{1,0:T(8,128)(2,1)} %keys_ref.1, bf16[512,1024]{1,0:T(8,128)(2,1)} %values_ref.1), custom_call_target="tpu_custom_call" | custom-call | tf_op jit(solution)/shard_map/pallas_call | solution.py:688
  39.7 1.3 %copy.6 = bf16[512,2048]{1,0:T(8,128)(2,1)} copy(bf16[512,2048]{1,0:T(8,128)(2,1)S(1)} %shard_map.46) | data formatting | bytes 4194304
